TPU v7x, 256 devices: a whole 4x4x8 slice. The times are simulated.
256 devices in a mesh: mp: 64 (over z, x, core), head: 4 (over y).
Axes of the slice: x: 4, y: 4, z: 8, core: 2. Of those that a mesh axis runs over, the one named last changes fastest.
Arguments:
- hidden: bfloat16 [8, 4096], replicated, may hold values from -6 to 6
- norm_gain: float32 [4096], replicated, may hold values from 0.25 to 1.75
- w_query: bfloat16 [4096, 4096], P('mp', 'head'), may hold values from -0.09375 to 0.09375
- enc_states: bfloat16 [8, 4096, 4096], P(None, 'mp'), may hold values from -6 to 6
- w_key: bfloat16 [4096, 4096], P('mp', 'head'), may hold values from -0.09375 to 0.09375
- w_value: bfloat16 [4096, 4096], P('mp', 'head'), may hold values from -0.09375 to 0.09375
- w_out: bfloat16 [4096, 4096], P('head', 'mp'), may hold values from -0.09375 to 0.09375
- bias_table: float32 [32, 64], P(None, 'head'), may hold values from -5 to 300
- buckets: int32 [8, 4096], P(None, 'mp'), may hold values from 0 to 31
- src_len: int32 [8], replicated, may hold values from 512 to 4096
Outputs:
- updated: bfloat16 [8, 4096], P(None, 'mp')
All inputs are finite; a program needn't handle non-finite values.
Results may differ from a plain program's by a relative error of at most 0.0049.
Values may be sent and summed in bfloat16 or wider, within the bound.
A program may use at most 128 MiB of HBM per device.

v0:
```python
import jax
import jax.numpy as jnp
from jax import lax
from jax.sharding import PartitionSpec as P

EPSILON = 1e-06
NEGATIVE = -1e30


def shards(
    hidden, norm_gain, w_query, enc_states, w_key, w_value, w_out, bias_table, buckets, src_len
):
    batch, src_local, _ = enc_states.shape
    rows, inner = w_key.shape
    heads = bias_table.shape[1]
    head_size = inner // heads
    me = lax.axis_index("mp")
    widened = hidden.astype(jnp.float32)
    mean_square = jnp.mean(widened * widened, axis=-1, keepdims=True)
    normed = (widened * lax.rsqrt(mean_square + EPSILON) * norm_gain).astype(jnp.bfloat16)
    mine = lax.dynamic_slice_in_dim(normed, me * rows, rows, 1)
    query = jnp.dot(mine, w_query, preferred_element_type=jnp.float32)
    query = lax.psum(query, "mp").astype(jnp.bfloat16).reshape(batch, heads, head_size)
    probe = jnp.einsum(
        "bhe,dhe->bhd",
        query,
        w_key.reshape(rows, heads, head_size),
        preferred_element_type=jnp.float32,
    )
    probe = (probe * float(head_size) ** (-0.5)).astype(jnp.bfloat16)
    probe = lax.all_gather(probe, "mp", axis=2, tiled=True)
    scores = jnp.einsum("bhd,bsd->bhs", probe, enc_states, preferred_element_type=jnp.float32)
    ids = jnp.arange(bias_table.shape[0], dtype=jnp.int32)
    one_hot = (buckets[:, :, None] == ids[None, None, :]).astype(jnp.float32)
    scores = scores + jnp.einsum(
        "bsk,kh->bhs", one_hot, bias_table, precision=lax.Precision.HIGHEST
    )
    positions = me * src_local + jnp.arange(src_local, dtype=jnp.int32)
    live = (positions[None, :] < src_len[:, None])[:, None, :]
    scores = jnp.where(live, scores, NEGATIVE)
    top = lax.pmax(jnp.max(scores, axis=-1), "mp")
    weights = jnp.where(live, jnp.exp(scores - top[:, :, None]), 0.0)
    total = lax.psum(jnp.sum(weights, axis=-1), "mp")
    mixed = jnp.einsum(
        "bhs,bsd->bhd", weights.astype(jnp.bfloat16), enc_states, preferred_element_type=jnp.float32
    )
    mixed = lax.psum_scatter(mixed, "mp", scatter_dimension=2, tiled=True)
    mixed = (mixed / total[:, :, None]).astype(jnp.bfloat16)
    context = jnp.einsum(
        "bhd,dhe->bhe",
        mixed,
        w_value.reshape(rows, heads, head_size),
        preferred_element_type=jnp.float32,
    )
    context = lax.psum(context, "mp").astype(jnp.bfloat16).reshape(batch, inner)
    out = lax.psum(jnp.dot(context, w_out, preferred_element_type=jnp.float32), "head")
    cols = w_out.shape[1]
    residual = lax.dynamic_slice_in_dim(widened, me * cols, cols, 1)
    return (out + residual).astype(jnp.bfloat16)


def solution(mesh):
    in_specs = (
        P(),
        P(),
        P("mp", "head"),
        P(None, "mp", None),
        P("mp", "head"),
        P("mp", "head"),
        P("head", "mp"),
        P(None, "head"),
        P(None, "mp"),
        P(),
    )
    return jax.shard_map(
        shards, mesh=mesh, in_specs=in_specs, out_specs=P(None, "mp"), check_vma=False
    )
```

profile of v0, /device:TPU:0, one launch (start us, length us, event | category | flops | bytes accessed | tf_op | source)
XLA Modules:
  0.0 922.8 jit_solution(14839864621208806205)
XLA Ops:
  6.5 0.0 copy-start
  6.5 0.0 all-gather.2.cloned.1.call-start
  6.5 0.9 convert_element_type.28
  7.4 1.0 multiply_reduce_fusion
  8.4 0.8 dynamic-slice
  9.2 0.0 copy-done
  9.2 0.2 fusion.19
  9.4 251.9 %psum.28 = bf16[8,1024]{1,0:T(8,128)(2,1)S(1)} all-reduce(f32[8,1024]{1,0:T(8,128)S(1)} %fusion.19), channel_id=1, replica_groups=mesh['mp'=64,'head'=4] {'mp'}, use_global_device_ids=true, to_apply=%region_1.0 | all-reduce | flops 8192 | bytes 49152 | tf_op jit(solution)/shard_map/psum | solution.py:23
  261.3 0.1 reshape.51
  261.4 1.1 reshape.52
  262.5 0.3 fusion.5
  262.7 0.8 copy.16
  263.5 0.0 all-gather.2.cloned.1.call-update
  263.6 0.0 reduce-scatter.4.cloned.1.call-start
  263.6 0.7 broadcast_compare_fusion
  264.4 0.0 copy-start.3
  264.4 0.0 copy-start.4
  264.4 77.1 %all-gather.2.cloned.1.call-done = bf16[8,16,4096]{1,0,2:T(8,128)(2,1)} async-done(((bf16[8,16,64]{1,0,2:T(8,128)(2,1)}), bf16[8,16,4096]{1,0,2:T(8,128)(2,1)}) %all-gather.2.cloned.1.call-update) | async-done | bytes 1048592 | tf_op jit(solution)/shard_map/all_gather | solution.py:31
  341.5 7.3 fusion
  348.8 0.0 copy-done.3
  348.8 0.0 copy-done.4
  348.8 0.3 fusion.24
  349.1 126.0 %pmax.7 = f32[8,16]{1,0:T(8,128)S(1)} all-reduce(f32[8,16]{1,0:T(8,128)S(1)} %get-tuple-element.5), channel_id=1, replica_groups=mesh['mp'=64,'head'=4] {'mp'}, use_global_device_ids=true, to_apply=%region_3.4 | all-reduce | flops 128 | bytes 1024 | tf_op jit(solution)/shard_map/pmax | solution.py:41
  475.1 2.9 fusion.11
  478.0 16.8 %copy.22 = f32[8,16,4096]{0,1,2:T(8,128)} copy(f32[8,16,4096]{2,1,0:T(8,128)S(1)} %fusion.11) | data formatting | bytes 4194304
  494.8 0.0 copy-start.1
  494.8 23.7 %reshape.56 = f32[4096,128]{1,0:T(8,128)} reshape(f32[4096,16,8]{2,1,0:T(8,128)} %bitcast.23) | data formatting | bytes 4194304
  518.5 0.0 copy-start.2
  518.5 0.0 reduce-scatter.4.cloned.1.call-update
  518.5 0.0 copy-done.1
  518.6 0.2 reshape.53
  518.7 0.2 fusion.9
  518.9 124.3 %psum.29 = f32[8,16]{1,0:T(8,128)S(1)} all-reduce(f32[8,16]{1,0:T(8,128)S(1)} %fusion.9), channel_id=1, replica_groups=mesh['mp'=64,'head'=4] {'mp'}, use_global_device_ids=true, to_apply=%region_6.7 | all-reduce | flops 128 | bytes 1024 | tf_op jit(solution)/shard_map/psum | solution.py:43
  643.2 0.1 copy.19
  643.3 13.6 %reduce-scatter.4.cloned.1.call-done = f32[64,128]{1,0:T(8,128)} async-done(((f32[4096,128]{1,0:T(8,128)}), f32[64,128]{1,0:T(8,128)}) %reduce-scatter.4.cloned.1.call-update) | async-done | bytes 32784
  656.9 1.0 reshape.57
  658.0 0.2 copy.23
  658.2 0.2 convolution_bitcast_fusion
  658.5 246.1 %psum.30 = bf16[8,16,64]{2,0,1:T(8,128)(2,1)S(1)} all-reduce(f32[8,16,64]{2,0,1:T(8,128)S(1)} %convolution_bitcast_fusion), channel_id=1, replica_groups=mesh['mp'=64,'head'=4] {'mp'}, use_global_device_ids=true, to_apply=%region_7.8 | all-reduce | flops 8192 | bytes 49152 | tf_op jit(solution)/shard_map/psum | solution.py:55
  904.6 0.1 reshape.54
  904.7 0.0 copy-done.2
  904.7 0.1 fusion.25
  904.9 10.5 %psum.31 = f32[8,64]{1,0:T(8,128)S(1)} all-reduce(f32[8,64]{1,0:T(8,128)S(1)} %fusion.25), channel_id=1, replica_groups=mesh['mp'=64,'head'=4] {'head'}, use_global_device_ids=true, to_apply=%region_8.9 | all-reduce | flops 512 | bytes 4096 | tf_op jit(solution)/shard_map/psum | solution.py:56
  915.3 0.7 add_convert_fusion
  (3 shorter events, 0.0 us)
Async XLA Ops:
  6.5 2.7 copy-start
  6.5 334.9 %all-gather.2.cloned.1.call-start = ((), (), s32[]{:S(2)}) async-start(), calls=%async_computation.1 | async-start | bytes 8519680 | tf_op jit(solution)/shard_map/all_gather | solution.py:31
  263.6 393.4 %reduce-scatter.4.cloned.1.call-start = ((), (), s32[]{:S(2)}) async-start(), calls=%async_computation.2 | async-start | bytes 2129920
  264.4 84.4 %copy-start.3 = (f32[32,16]{0,1:T(8,128)S(1)}, f32[32,16]{0,1:T(8,128)}, u32[]{:S(2)}) copy-start(f32[32,16]{0,1:T(8,128)} %param.17) | copy-start | bytes 6148
  264.4 84.4 %copy-start.4 = (s32[8,64]{1,0:T(8,128)S(1)}, s32[8,64]{1,0:T(8,128)}, u32[]{:S(2)}) copy-start(s32[8,64]{1,0:T(8,128)} %param.18) | copy-start | bytes 6148
  494.8 23.7 %copy-start.1 = (bf16[64,1024]{1,0:T(8,128)(2,1)S(1)}, bf16[64,1024]{1,0:T(8,128)(2,1)}, u32[]{:S(2)}) copy-start(bf16[64,1024]{1,0:T(8,128)(2,1)} %param.15) | copy-start | bytes 393220
  518.5 386.2 %copy-start.2 = (bf16[1024,64]{0,1:T(8,128)(2,1)S(1)}, bf16[1024,64]{0,1:T(8,128)(2,1)}, u32[]{:S(2)}) copy-start(bf16[1024,64]{0,1:T(8,128)(2,1)} %param.16) | copy-start | bytes 393220
Sparse Core Ops, SparseCore 0:
  263.7 77.7 all-gather.1
  518.7 138.2 reduce-scatter.3
where the time goes:
time: 924 us; the launch traced here: 923 us
  blocking collectives  759 us (82%)
  waiting for transfers between devices  90.8 us (10%)
  local copies, waits for them, and re-layouts  45 us (5%)
  between operations  13.5 us (1%)
  matrix products  11.3 us (1%)
    psum x1, blocking collectives, shards(): lax.psum(query, 'mp').astype(jnp.bfloat16).reshape(batch, heads, head_size)  252 us
    psum x1, blocking collectives, shards(): context = lax.psum(context, 'mp').astype(jnp.bfloat16).reshape(batch, inner)  246 us
    pmax x1, blocking collectives, shards(): top = lax.pmax(jnp.max(scores, axis=-1), 'mp')  126 us
    psum x1, blocking collectives, shards(): total = lax.psum(jnp.sum(weights, axis=-1), 'mp')  124 us
    all_gather x1, waiting for transfers between devices, shards(): probe = lax.all_gather(probe, 'mp', axis=2, tiled=True)  77.1 us
    unnamed x14, local copies, waits for them, and re-layouts  41.8 us
  transfers between devices with their start and end apart: 2, of which 2 were waited for; matrix products, arithmetic and copies ran while one was open for 0% of the time, Pallas kernels for 0%

commit v1 on v0

--- a/solution.py
+++ b/solution.py
@@ -28,7 +28,9 @@
         preferred_element_type=jnp.float32,
     )
     probe = (probe * float(head_size) ** (-0.5)).astype(jnp.bfloat16)
-    probe = lax.all_gather(probe, "mp", axis=2, tiled=True)
+    probe = jnp.concatenate(
+        lax.all_to_all(jnp.stack([probe] * lax.axis_size("mp")), "mp", 0, 0), axis=2
+    )
     scores = jnp.einsum("bhd,bsd->bhs", probe, enc_states, preferred_element_type=jnp.float32)
     ids = jnp.arange(bias_table.shape[0], dtype=jnp.int32)
     one_hot = (buckets[:, :, None] == ids[None, None, :]).astype(jnp.float32)

time: 924 us -> 884 us (0.957)
  waiting for transfers between devices: 90.8 us -> 42.8 us
  local copies, waits for them, and re-layouts: 45 us -> 54.4 us
    all_gather x1 -> x0, waiting for transfers between devices: 77.1 us -> none  [shards(): probe = lax.all_gather(probe, 'mp', axis=2, tiled=True)]
    all_to_all x0 -> x1, waiting for transfers between devices: none -> 28.7 us  [shards(): lax.all_to_all(jnp.stack([probe] * lax.axis_size('mp')), 'mp', 0, 0)]
    unnamed x14 -> x18, local copies, waits for them, and re-layouts: 41.8 us -> 45.5 us
where the time goes in v1:
time: 884 us; the launch traced here: 883 us
  blocking collectives  758 us (86%)
  local copies, waits for them, and re-layouts  54.4 us (6%)
  waiting for transfers between devices  42.8 us (5%)
  between operations  13.5 us (2%)
    psum x1, blocking collectives, shards(): lax.psum(query, 'mp').astype(jnp.bfloat16).reshape(batch, heads, head_size)  252 us
    psum x1, blocking collectives, shards(): context = lax.psum(context, 'mp').astype(jnp.bfloat16).reshape(batch, inner)  246 us
    pmax x1, blocking collectives, shards(): top = lax.pmax(jnp.max(scores, axis=-1), 'mp')  125 us
    psum x1, blocking collectives, shards(): total = lax.psum(jnp.sum(weights, axis=-1), 'mp')  124 us
    unnamed x18, local copies, waits for them, and re-layouts  45.5 us
    all_to_all x1, waiting for transfers between devices, shards(): lax.all_to_all(jnp.stack([probe] * lax.axis_size('mp')), 'mp', 0, 0)  28.7 us
  transfers between devices with their start and end apart: 2, of which 2 were waited for; matrix products, arithmetic and copies ran while one was open for 0% of the time, Pallas kernels for 0%

profile of v1, /device:TPU:0, one launch (start us, length us, event | category | flops | bytes accessed | tf_op | source)
XLA Modules:
  0.0 883.5 jit_solution(15381726098975800439)
XLA Ops:
  6.5 0.0 copy-start
  6.5 0.9 convert_element_type.28
  7.4 1.0 multiply_reduce_fusion
  8.4 0.8 dynamic-slice
  9.2 0.0 copy-done
  9.2 0.0 copy-start.5
  9.2 0.2 fusion.17
  9.4 251.9 %psum.28 = bf16[8,1024]{1,0:T(8,128)(2,1)S(1)} all-reduce(f32[8,1024]{1,0:T(8,128)S(1)} %fusion.17), channel_id=1, replica_groups=mesh['mp'=64,'head'=4] {'mp'}, use_global_device_ids=true, to_apply=%region_1.0 | all-reduce | flops 8192 | bytes 49152 | tf_op jit(solution)/shard_map/psum | solution.py:23
  261.3 0.1 reshape.59
  261.4 1.1 reshape.60
  262.5 0.2 fusion.3
  262.7 0.5 stack.2
  263.3 2.3 reshape.68
  265.6 4.7 all-to-all-start
  270.2 0.0 reduce-scatter.4.cloned.1.call-start
  270.3 0.0 copy-done.5
  270.3 0.1 broadcast_compare_fusion
  270.4 28.7 %all-to-all-done = bf16[64,2,4096]{2,1,0:T(2,128)(2,1)S(1)} async-done(((bf16[64,2,4096]{2,1,0:T(2,128)(2,1)}), bf16[64,2,4096]{2,1,0:T(2,128)(2,1)S(1)}, u32[]{:S(2)}, u32[]{:S(2)}) %all-to-all-start) | async-done | bytes 1048608 | tf_op jit(solution)/shard_map/all_to_all | solution.py:32
  299.1 1.3 reshape.69
  300.4 2.7 copy.23
  303.2 0.0 copy-start.3
  303.2 0.0 copy-start.4
  303.2 3.3 reshape.62
  306.5 3.4 fusion.23
  309.9 0.0 copy-done.3
  309.9 0.0 copy-done.4
  309.9 0.3 fusion.22
  310.2 125.2 %pmax.7 = f32[8,16]{1,0:T(8,128)S(1)} all-reduce(f32[8,16]{1,0:T(8,128)S(1)} %get-tuple-element.5), channel_id=1, replica_groups=mesh['mp'=64,'head'=4] {'mp'}, use_global_device_ids=true, to_apply=%region_3.4 | all-reduce | flops 128 | bytes 1024 | tf_op jit(solution)/shard_map/pmax | solution.py:43
  435.4 2.9 fusion.9
  438.3 16.8 %copy.28 = f32[8,16,4096]{0,1,2:T(8,128)} copy(f32[8,16,4096]{2,1,0:T(8,128)S(1)} %fusion.9) | data formatting | bytes 4194304
  455.1 0.0 copy-start.1
  455.1 23.7 %reshape.66 = f32[4096,128]{1,0:T(8,128)} reshape(f32[4096,16,8]{2,1,0:T(8,128)} %bitcast.27) | data formatting | bytes 4194304
  478.8 0.0 reduce-scatter.4.cloned.1.call-update
  478.8 0.0 copy-done.1
  478.8 0.2 reshape.63
  479.0 0.2 fusion.7
  479.2 124.2 %psum.29 = f32[8,16]{1,0:T(8,128)S(1)} all-reduce(f32[8,16]{1,0:T(8,128)S(1)} %fusion.7), channel_id=1, replica_groups=mesh['mp'=64,'head'=4] {'mp'}, use_global_device_ids=true, to_apply=%region_6.7 | all-reduce | flops 128 | bytes 1024 | tf_op jit(solution)/shard_map/psum | solution.py:45
  603.4 0.1 copy.25
  603.5 14.1 %reduce-scatter.4.cloned.1.call-done = f32[64,128]{1,0:T(8,128)} async-done(((f32[4096,128]{1,0:T(8,128)}), f32[64,128]{1,0:T(8,128)}) %reduce-scatter.4.cloned.1.call-update) | async-done | bytes 32784
  617.6 1.0 reshape.67
  618.6 0.2 copy.29
  618.9 0.2 convolution_bitcast_fusion
  619.1 246.1 %psum.30 = bf16[8,16,64]{2,0,1:T(8,128)(2,1)S(1)} all-reduce(f32[8,16,64]{2,0,1:T(8,128)S(1)} %convolution_bitcast_fusion), channel_id=1, replica_groups=mesh['mp'=64,'head'=4] {'mp'}, use_global_device_ids=true, to_apply=%region_7.8 | all-reduce | flops 8192 | bytes 49152 | tf_op jit(solution)/shard_map/psum | solution.py:57
  865.3 0.1 reshape.64
  865.4 0.0 copy-done.2
  865.4 0.1 fusion.24
  865.5 10.5 %psum.31 = f32[8,64]{1,0:T(8,128)S(1)} all-reduce(f32[8,64]{1,0:T(8,128)S(1)} %fusion.24), channel_id=1, replica_groups=mesh['mp'=64,'head'=4] {'head'}, use_global_device_ids=true, to_apply=%region_8.9 | all-reduce | flops 512 | bytes 4096 | tf_op jit(solution)/shard_map/psum | solution.py:58
  876.0 0.7 add_convert_fusion
  (5 shorter events, 0.0 us)
Async XLA Ops:
  6.5 2.7 copy-start
  9.2 261.1 %copy-start.5 = (s32[8]{0:T(128)S(1)}, s32[8]{0:T(128)}, u32[]{:S(2)}) copy-start(s32[8]{0:T(128)} %param.19) | copy-start | bytes 100
  265.6 33.5 %all-to-all-start = ((bf16[64,2,4096]{2,1,0:T(2,128)(2,1)}), bf16[64,2,4096]{2,1,0:T(2,128)(2,1)S(1)}, u32[]{:S(2)}, u32[]{:S(2)}) async-start(bf16[64,2,4096]{2,1,0:T(2,128)(2,1)} %reshape.68), calls=%async_computation | async-start | bytes 2097152 | tf_op jit(solution)/shard_map/all_to_all | solution.py:32
  270.2 347.3 %reduce-scatter.4.cloned.1.call-start = ((), (), s32[]{:S(2)}) async-start(), calls=%async_computation.2 | async-start | bytes 2129920
  303.2 6.7 copy-start.3
  303.2 6.7 copy-start.4
  455.1 23.7 %copy-start.1 = (bf16[64,1024]{1,0:T(8,128)(2,1)S(1)}, bf16[64,1024]{1,0:T(8,128)(2,1)}, u32[]{:S(2)}) copy-start(bf16[64,1024]{1,0:T(8,128)(2,1)} %param.15) | copy-start | bytes 393220
  478.8 386.6 %copy-start.2 = (bf16[1024,64]{0,1:T(8,128)(2,1)S(1)}, bf16[1024,64]{0,1:T(8,128)(2,1)}, u32[]{:S(2)}) copy-start(bf16[1024,64]{0,1:T(8,128)(2,1)} %param.16) | copy-start | bytes 393220
Sparse Core Ops, SparseCore 0:
  479.0 138.5 reduce-scatter.3
